TPU v7x, 32 devices: a whole 2x2x4 slice. The times are simulated.
32 devices in a mesh: sa: 4 (over y, core), sb: 8 (over z, x).
Axes of the slice: x: 2, y: 2, z: 4, core: 2. Of those that a mesh axis runs over, the one named last changes fastest.
Arguments:
- queries: bfloat16 [1024, 1024], P(('sa', 'sb')), may hold values from -6 to 6
- out_grad: bfloat16 [1024, 1024], P(('sa', 'sb')), may hold values from -6144 to 6144
- forward_out: bfloat16 [1024, 1024], P(('sa', 'sb')), may hold values from -3 to 3
- lse_shift: float32 [1024, 8], P(('sa', 'sb')), may hold values from 0.2 to 1
- key_rows: bfloat16 [32768, 256], P(('sa', 'sb')), may hold values from -7 to 7
- value_rows: bfloat16 [32768, 256], P(('sa', 'sb')), may hold values from -6 to 6
Outputs:
- query_grad: float32 [1024, 1024], P(('sa', 'sb'))
- key_grad: bfloat16 [32768, 256], P(('sa', 'sb'))
- value_grad: bfloat16 [32768, 256], P(('sa', 'sb'))
All inputs are finite; a program needn't handle non-finite values.
Results may differ from a plain program's by a relative error of at most 0.0097.
Values may be sent and summed in bfloat16 or wider, within the bound.
A program may use at most 64 MiB of HBM per device.

v0:
```python
import functools
import math

import jax
import jax.numpy as jnp
from jax import lax
from jax.experimental import pallas as pl
from jax.experimental.pallas import tpu as pltpu
from jax.sharding import PartitionSpec as P

QH = 8
KVH = 2
HEAD_DIM = 128
MESH = pl.DeviceIdType.MESH
BF = jnp.bfloat16
F32 = jnp.float32
AXES = ("sa", "sb")


def grid_of(sa, sb):
    inner = 2 ** (int(math.log2(sb)) // 2)
    return sa // 2, sb // inner, inner


class Place:
    def __init__(self, dims):
        self.dims = dims
        sa, sb = lax.axis_index("sa"), lax.axis_index("sb")
        self.core = sa % 2
        self.at = (sa // 2, sb // dims[2], sb % dims[2])

    def other(self, axis, step):
        at = list(self.at)
        at[axis] = (at[axis] + step) % self.dims[axis]
        return tuple(at)

    def back(self, offset):
        return tuple((p + n - o) % n for p, n, o in zip(self.at, self.dims, offset))

    def device(self, at):
        return (at[0] * 2 + self.core, at[1] * self.dims[2] + at[2])

    def partner(self):
        return (self.at[0] * 2 + 1 - self.core, lax.axis_index("sb"))

    def slot(self, at):
        return (at[0] * self.dims[1] + at[1]) * self.dims[2] + at[2]

    def greet(self):
        barrier = pltpu.get_barrier_semaphore()
        peers = [self.partner()]
        for axis in range(3):
            for step in range(1, self.dims[axis]):
                peers.append(self.device(self.other(axis, step)))
        for peer in peers:
            pl.semaphore_signal(barrier, inc=1, device_id=peer, device_id_type=MESH)
        pl.semaphore_wait(barrier, len(peers))


def pieces(x):
    hi = x.astype(BF)
    rest = x - hi.astype(F32)
    mid = rest.astype(BF)
    low = (rest - mid.astype(F32)).astype(BF)
    return hi, mid, low


def relay_sends(dims):
    na, nb, nd = dims
    line, corner = [], []
    for b in range(1, nb):
        line += [((0, b, 0), 2, step) for step in range(1, nd)]
        line += [((0, b, 0), 0, step) for step in range(1, na)]
    for b in range(nb):
        corner += [("x", (0, b, d), 0, s) for d in range(1, nd) for s in range(1, na)]
        corner += [("d", (a, b, 0), 2, s) for a in range(1, na) for s in range(1, nd)]
    return line, corner


def first_sends(dims):
    along = [(1, step) for step in range(1, dims[1])]
    across = [(2, step) for step in range(1, dims[2])] + [(0, step) for step in range(1, dims[0])]
    return along, across


def counts(dims):
    na, nb, nd = dims
    line, corner = relay_sends(dims)
    along, across = first_sends(dims)
    own = len(along) + len(across) + len(line)
    x_diag = sum(1 for c in corner if c[0] == "x")
    gathered = 5 * own + 3 * x_diag + 2 * (len(corner) - x_diag)
    reduced = 2 * (2 * (na - 1) + 2 * (nd - 1) + (nb - 1))
    return gathered, reduced


def whole_kernel(dims, total_keys, tile, q_ref, d_ref, o_ref, lse_ref, k_ref, v_ref,
                 dq_out, dk_out, dv_out,
                 qa, da, xa, aux_ref, ks, va, half, halfr, acc, part, dks, dvs, kvr,
                 r1a, r1b, t1a, t1b, r2a, r2b, t2, r3,
                 send_sem, q_sem, d_sem, x_sem, kv_send, kv_recv, red_send, red_recv):
    na, nb, nd = dims
    members = na * nb * nd
    place = Place(dims)
    pa, pb, pd = place.at
    rows = q_ref.shape[0]
    keys = k_ref.shape[0]
    group = q_ref.shape[1] // KVH
    per_group = QH // KVH
    me = place.slot(place.at)
    scale = 1.0 / math.sqrt(HEAD_DIM)
    place.greet()
    line, corner = relay_sends(dims)
    along, across = first_sends(dims)
    origin = (0, 0, 0)

    partner_copies = []

    def to_partner(src, dst):
        n = len(partner_copies)
        copy = pltpu.make_async_remote_copy(
            src_ref=src, dst_ref=dst, send_sem=kv_send.at[n], recv_sem=kv_recv.at[n],
            device_id=place.partner(), device_id_type=MESH)
        copy.start()
        partner_copies.append(copy)
        return copy

    to_partner(k_ref, ks.at[1])
    to_partner(v_ref, va.at[1])

    def flat(offset):
        return (offset[0] * nb + offset[1]) * nd + offset[2]

    def places(kind, slot, offset):
        if kind == "x":
            return xa.at[slot], x_sem.at[flat(offset)]
        c = int(kind[1])
        buf, sem = (qa, q_sem) if kind[0] == "q" else (da, d_sem)
        return buf.at[c, slot], sem.at[c, flat(offset)]

    started = []

    def send(kind, offset, axis, step):
        slot = place.slot(place.back(offset))
        there = list(offset)
        there[axis] = (there[axis] + step) % dims[axis]
        ref, sem = places(kind, slot, there)
        src = ref
        if offset == origin and kind != "x":
            src = (q_ref if kind[0] == "q" else d_ref).at[:, pl.ds(int(kind[1]) * group, group)]
        copy = pltpu.make_async_remote_copy(
            src_ref=src, dst_ref=ref, send_sem=send_sem.at[len(started)], recv_sem=sem,
            device_id=place.device(place.other(axis, step)), device_id_type=MESH)
        copy.start()
        started.append(copy)

    arrived = set()

    def need(kind, offset):
        if offset == origin or (kind, offset) in arrived:
            return
        arrived.add((kind, offset))
        ref, sem = places(kind, place.slot(place.back(offset)), offset)
        pltpu.make_async_remote_copy(
            src_ref=ref, dst_ref=ref, send_sem=send_sem.at[0], recv_sem=sem,
            device_id=place.partner(), device_id_type=MESH).wait_recv()

    def send_first(kind, directions):
        for axis, step in directions:
            send(kind, origin, axis, step)

    def send_line(kinds):
        for offset, axis, step in line:
            for kind in kinds:
                need(kind, offset)
                send(kind, offset, axis, step)

    def send_corner(kinds):
        for which, offset, axis, step in corner:
            for kind in kinds:
                if (kind[0] == "d") == (which == "d"):
                    need(kind, offset)
                    send(kind, offset, axis, step)

    def need_all(kinds):
        for a in range(na):
            for b in range(nb):
                for d in range(nd):
                    for kind in kinds:
                        need(kind, (a, b, d))

    for kind in ("q0", "d0"):
        send_first(kind, along + across)

    lane = lax.broadcasted_iota(jnp.int32, (rows, HEAD_DIM), 1)
    aux = jnp.zeros((rows, HEAD_DIM), F32)
    for head in range(QH):
        cols = pl.ds(head * HEAD_DIM, HEAD_DIM)
        product = d_ref[:, cols].astype(F32) * o_ref[:, cols].astype(F32)
        delta = jnp.sum(product, axis=1, keepdims=True)
        offset = (lse_ref[:, head:head + 1] + math.log(total_keys)) * (1.0 / scale)
        for at, value in ((0, offset), (3 * QH, delta)):
            for n, piece in enumerate(pieces(value)):
                aux = jnp.where(lane == at + 3 * head + n, piece.astype(F32), aux)
    xa[me, pl.ds(0, rows), :] = aux.astype(BF)
    chunk = 128

    def add_rows(n, total):
        block = k_ref[pl.ds(pl.multiple_of(n * chunk, chunk), chunk), :].astype(F32)
        return total + jnp.sum(block, axis=0, keepdims=True)

    key_sum = lax.fori_loop(0, keys // chunk, add_rows, jnp.zeros((1, KVH * HEAD_DIM), F32))
    row = lax.broadcasted_iota(jnp.int32, (16, HEAD_DIM), 0)
    small = jnp.zeros((16, HEAD_DIM), F32)
    for n, piece in enumerate(pieces(key_sum)):
        for c in range(KVH):
            term = piece[:, c * HEAD_DIM:(c + 1) * HEAD_DIM].astype(F32)
            small = jnp.where(row == 2 * n + c, term, small)
    xa[me, pl.ds(rows, 16), :] = small.astype(BF)
    send_first("x", along + across)
    for kind in ("q1", "d1"):
        send_first(kind, along)
    for c in range(KVH):
        qa[c, me] = q_ref[:, pl.ds(c * group, group)]
        da[c, me] = d_ref[:, pl.ds(c * group, group)]
    va[0] = v_ref[...]
    send_line(("x",))
    send_line(("q0", "d0"))
    send_corner(("x",))
    send_corner(("q0", "d0"))
    for kind in ("q1", "d1"):
        send_first(kind, across)

    need_all(("x",))
    half_sum = jnp.zeros((16, HEAD_DIM), F32)
    for g in range(members):
        half_sum = half_sum + xa[g, pl.ds(rows, 16), :].astype(F32)
        aux_ref[pl.ds(g * rows, rows), :] = xa[g, pl.ds(0, rows), :]
    half[...] = half_sum
    to_partner(half, halfr)
    send_line(("q1", "d1"))
    for copy in partner_copies:
        copy.wait_recv()
    both = half[...] + halfr[...]
    for c in range(KVH):
        cols = pl.ds(c * HEAD_DIM, HEAD_DIM)
        mean = (both[c:c + 1] + both[c + 2:c + 3] + both[c + 4:c + 5]) / total_keys

        def smooth(n, carry):
            at = pl.ds(pl.multiple_of(n * chunk, chunk), chunk)
            ks[0, at, cols] = (k_ref[at, cols].astype(F32) - mean).astype(BF)
            ks[1, at, cols] = (ks[1, at, cols].astype(F32) - mean).astype(BF)
            return carry

        lax.fori_loop(0, keys // chunk, smooth, 0)
    need_all(("q0", "d0"))

    nt = (((1,), (1,)), ((), ()))
    tiles = keys // tile
    key_lane = lax.broadcasted_iota(jnp.int32, (tile, HEAD_DIM), 1)

    def attend(c, side, first):
        cols = pl.ds(c * HEAD_DIM, HEAD_DIM)

        def one(t, carry):
            at = pl.ds(pl.multiple_of(t * tile, tile), tile)
            kt = ks[side, at, cols]
            vt = va[side, at, cols]
            aux_all = aux_ref[...]
            dk = jnp.zeros((tile, HEAD_DIM), F32)
            dv = jnp.zeros((tile, HEAD_DIM), F32)
            for g in range(per_group):
                head_cols = pl.ds(g * HEAD_DIM, HEAD_DIM)
                heads_q = qa[c, :, :, head_cols].reshape(members * rows, HEAD_DIM)
                heads_d = da[c, :, :, head_cols].reshape(members * rows, HEAD_DIM)
                low = 3 * (c * per_group + g)
                minus_s = jnp.where((key_lane >= low) & (key_lane < low + 3), -1.0, 0.0)
                low = low + 3 * QH
                minus_d = jnp.where((key_lane >= low) & (key_lane < low + 3), -1.0, 0.0)
                s = lax.dot_general(jnp.concatenate([kt, minus_s.astype(BF)], 1),
                                    jnp.concatenate([heads_q, aux_all], 1), nt,
                                    preferred_element_type=F32)
                dp = lax.dot_general(jnp.concatenate([vt, minus_d.astype(BF)], 1),
                                     jnp.concatenate([heads_d, aux_all], 1), nt,
                                     preferred_element_type=F32)
                prob = jnp.exp2(s * (scale * math.log2(math.e)))
                dv = dv + jnp.dot(prob.astype(BF), heads_d, preferred_element_type=F32)
                ds = (prob * dp).astype(BF)
                dk = dk + jnp.dot(ds, heads_q, preferred_element_type=F32)
                acc[:, head_cols] += lax.dot_general(
                    ds, kt, (((0,), (0,)), ((), ())), preferred_element_type=F32)
            dks[c, side, at, :] = (dk * scale).astype(BF)
            dvs[c, side, at, :] = dv.astype(BF)
            return carry

        if first:
            acc[...] = jnp.zeros(acc.shape, F32)
        lax.fori_loop(0, tiles, one, 0)

    def finish(c):
        part[c] = (acc[...] * scale).reshape(na, nb, nd, rows, group).astype(BF)

    mid = group // 2
    left, right = pl.ds(0, mid), pl.ds(mid, mid)
    reduced = []

    def red(src, dst, to):
        n = len(reduced)
        copy = pltpu.make_async_remote_copy(
            src_ref=src, dst_ref=dst, send_sem=red_send.at[n], recv_sem=red_recv.at[n],
            device_id=place.device(to), device_id_type=MESH)
        copy.start()
        reduced.append(copy)
        return copy

    def stage1(c):
        stage = []
        for s in range(1, nd):
            to = place.other(2, s)
            stage.append(red(part.at[c, :, :, to[2], :, left], r1a.at[c, s - 1], to))
        for s in range(1, na):
            to = place.other(0, s)
            stage.append(red(part.at[c, to[0], :, :, :, right], r1b.at[c, s - 1], to))
        return stage

    def stage2(c, stage):
        for copy in stage:
            copy.wait_recv()
        for i in range(na):
            for j in range(nb):
                total = part[c, i, j, pd, :, left].astype(F32)
                for s in range(nd - 1):
                    total = total + r1a[c, s, i, j].astype(F32)
                t1a[c, i, j] = total.astype(BF)
        for j in range(nb):
            for i in range(nd):
                total = part[c, pa, j, i, :, right].astype(F32)
                for s in range(na - 1):
                    total = total + r1b[c, s, j, i].astype(F32)
                t1b[c, i, j] = total.astype(BF)
        stage = []
        for s in range(1, na):
            to = place.other(0, s)
            stage.append(red(t1a.at[c, to[0]], r2a.at[c, s - 1], to))
        for s in range(1, nd):
            to = place.other(2, s)
            stage.append(red(t1b.at[c, to[2]], r2b.at[c, s - 1], to))
        return stage

    def stage3(c, stage):
        for copy in stage:
            copy.wait_recv()
        for j in range(nb):
            total = t1a[c, pa, j].astype(F32)
            for s in range(na - 1):
                total = total + r2a[c, s, j].astype(F32)
            t2[c, j, :, left] = total.astype(BF)
            total = t1b[c, pd, j].astype(F32)
            for s in range(nd - 1):
                total = total + r2b[c, s, j].astype(F32)
            t2[c, j, :, right] = total.astype(BF)
        stage = []
        for s in range(1, nb):
            to = place.other(1, s)
            stage.append(red(t2.at[c, to[1]], r3.at[c, s - 1], to))
        return stage

    def last(c, stage):
        for copy in stage:
            copy.wait_recv()
        total = t2[c, pb].astype(F32)
        for s in range(nb - 1):
            total = total + r3[c, s].astype(F32)
        dq_out[:, pl.ds(c * group, group)] = total

    kv = []
    for c in range(KVH):
        attend(c, 1, True)
        kv.append(to_partner(dks.at[c, 1], kvr.at[c, 0]))
        kv.append(to_partner(dvs.at[c, 1], kvr.at[c, 1]))
        if c == 0:
            send_corner(("q1", "d1"))
        else:
            stage = stage2(0, stage)
        attend(c, 0, False)
        finish(c)
        if c == 0:
            stage = stage1(0)
            need_all(("q1", "d1"))
    ending = stage1(1)
    stage = stage3(0, stage)

    for copy in kv:
        copy.wait_recv()

    def add_part(n, carry):
        at = pl.ds(pl.multiple_of(n * chunk, chunk), chunk)
        for c in range(KVH):
            cols = pl.ds(c * HEAD_DIM, HEAD_DIM)
            for out, mine, where in ((dk_out, dks, 0), (dv_out, dvs, 1)):
                out[at, cols] = (mine[c, 0, at, :].astype(F32)
                                 + kvr[c, where, at, :].astype(F32)).astype(BF)
        return carry

    lax.fori_loop(0, keys // chunk, add_part, 0)
    ending = stage2(1, ending)
    last(0, stage)
    ending = stage3(1, ending)
    last(1, ending)
    for copy in started + partner_copies + reduced:
        copy.wait_send()


def local(dims, q, d, o, lse, k, v):
    na, nb, nd = dims
    members = na * nb * nd
    rows, width = q.shape
    keys, kw = k.shape
    group, mid = width // KVH, width // KVH // 2
    tile = min(512, keys)
    gathered, reduced = counts(dims)
    vmem = pl.BlockSpec(memory_space=pltpu.VMEM)
    ma, mb, md = max(na - 1, 1), max(nb - 1, 1), max(nd - 1, 1)
    sem = pltpu.SemaphoreType.DMA
    return pl.pallas_call(
        functools.partial(whole_kernel, dims, keys * members * 2, tile),
        name="whole",
        out_shape=(
            jax.ShapeDtypeStruct((rows, width), F32),
            jax.ShapeDtypeStruct((keys, kw), BF),
            jax.ShapeDtypeStruct((keys, kw), BF),
        ),
        in_specs=[vmem] * 6,
        out_specs=(vmem,) * 3,
        scratch_shapes=[
            pltpu.VMEM((KVH, members, rows, group), BF),
            pltpu.VMEM((KVH, members, rows, group), BF),
            pltpu.VMEM((members, rows + 16, HEAD_DIM), BF),
            pltpu.VMEM((members * rows, HEAD_DIM), BF),
            pltpu.VMEM((2, keys, kw), BF),
            pltpu.VMEM((2, keys, kw), BF),
            pltpu.VMEM((16, HEAD_DIM), F32),
            pltpu.VMEM((16, HEAD_DIM), F32),
            pltpu.VMEM((members * rows, group), F32),
            pltpu.VMEM((KVH, na, nb, nd, rows, group), BF),
            pltpu.VMEM((KVH, 2, keys, HEAD_DIM), BF),
            pltpu.VMEM((KVH, 2, keys, HEAD_DIM), BF),
            pltpu.VMEM((KVH, 2, keys, HEAD_DIM), BF),
            pltpu.VMEM((KVH, md, na, nb, rows, mid), BF),
            pltpu.VMEM((KVH, ma, nb, nd, rows, mid), BF),
            pltpu.VMEM((KVH, na, nb, rows, mid), BF),
            pltpu.VMEM((KVH, nd, nb, rows, mid), BF),
            pltpu.VMEM((KVH, ma, nb, rows, mid), BF),
            pltpu.VMEM((KVH, md, nb, rows, mid), BF),
            pltpu.VMEM((KVH, nb, rows, group), BF),
            pltpu.VMEM((KVH, mb, rows, group), BF),
            sem((gathered,)),
            sem((KVH, members)),
            sem((KVH, members)),
            sem((members,)),
            sem((3 + 2 * KVH,)),
            sem((3 + 2 * KVH,)),
            sem((reduced,)),
            sem((reduced,)),
        ],
        compiler_params=pltpu.CompilerParams(
            collective_id=0, has_side_effects=True, vmem_limit_bytes=60 * 1024 * 1024),
    )(q, d, o, lse, k, v)


def solution(mesh):
    dims = grid_of(mesh.shape["sa"], mesh.shape["sb"])
    spec = P(("sa", "sb"), None)
    return jax.shard_map(functools.partial(local, dims), mesh=mesh, in_specs=(spec,) * 6,
                         out_specs=(spec,) * 3, check_vma=False)
```

profile of v0, /device:TPU:0, one launch (start us, length us, event | category | flops | bytes accessed | tf_op | source)
XLA Modules:
  0.0 74.0 jit_solution(16219540101710137829)
XLA Ops:
  0.6 1.4 %copy.9.lse_ref = f32[32,8]{1,0:T(8,128)} copy(f32[32,8]{0,1:T(8,128)} %param.9) | data formatting | bytes 2048 | tf_op args[3]
  2.0 67.7 %whole.1 = (f32[32,1024]{1,0:T(8,128)}, bf16[1024,256]{1,0:T(8,128)(2,1)}, bf16[1024,256]{1,0:T(8,128)(2,1)}) custom-call(bf16[32,1024]{1,0:T(8,128)(2,1)} %q_ref.1, bf16[32,1024]{1,0:T(8,128)(2,1)} %d_ref.1, bf16[32,1024]{1,0:T(8,128)(2,1)} %o_ref.1, f32[32,8]{1,0:T(8,128)} %copy.9.lse_ref, bf16[1024,256]{1,0:T(8,128)(2,1)} %k_ref.1, bf16[1024,256]{1,0:T(8,128)(2,1)} %v_ref.1), custom_call_target="tpu_custom_call" | custom-call | tf_op jit(solution)/shard_map/whole/pallas_call | solution.py:425
  69.7 1.6 %copy.13 = f32[32,1024]{1,0:T(8,128)} copy(f32[32,1024]{1,0:T(8,128)} %get-tuple-element.6) | data formatting | bytes 262144
  71.3 0.0 copy-start
  71.3 1.9 %copy.14 = bf16[1024,256]{1,0:T(8,128)(2,1)} copy(bf16[1024,256]{1,0:T(8,128)(2,1)} %get-tuple-element.7) | data formatting | bytes 1048576
  73.2 0.0 copy-done
  73.2 0.8 %copy.15 = bf16[1024,256]{1,0:T(8,128)(2,1)} copy(bf16[1024,256]{1,0:T(8,128)(2,1)S(1)} %copy-done) | data formatting | bytes 1048576
Async XLA Ops:
  71.3 1.9 %copy-start = (bf16[1024,256]{1,0:T(8,128)(2,1)S(1)}, bf16[1024,256]{1,0:T(8,128)(2,1)}, u32[]{:S(2)}) copy-start(bf16[1024,256]{1,0:T(8,128)(2,1)} %get-tuple-element.8) | copy-start | bytes 1572868
where the time goes:
time: 74.2 us; the launch traced here: 74 us
  Pallas kernels  67.7 us (91%)
  local copies, waits for them, and re-layouts  5.66 us (8%)
    pallas_call x1, Pallas kernels, local(): pl.pallas_call(functools.partial(whole_kernel, dims, keys * members * 2,...  67.7 us
    unnamed x6, local copies, waits for them, and re-layouts  5.66 us

commit v1 on v0

v1 whole, which is shorter than its diff:
```python
import functools
import math

import jax
import jax.numpy as jnp
from jax import lax
from jax.experimental import pallas as pl
from jax.experimental.pallas import tpu as pltpu
from jax.sharding import PartitionSpec as P

QH = 8
KVH = 2
HEAD_DIM = 128
MESH = pl.DeviceIdType.MESH
BF = jnp.bfloat16
F32 = jnp.float32
AXES = ("sa", "sb")


def grid_of(sa, sb):
    inner = 2 ** (int(math.log2(sb)) // 2)
    return sa // 2, sb // inner, inner


class Place:
    def __init__(self, dims):
        self.dims = dims
        sa, sb = lax.axis_index("sa"), lax.axis_index("sb")
        self.core = sa % 2
        self.at = (sa // 2, sb // dims[2], sb % dims[2])

    def other(self, axis, step):
        at = list(self.at)
        at[axis] = (at[axis] + step) % self.dims[axis]
        return tuple(at)

    def back(self, offset):
        return tuple((p + n - o) % n for p, n, o in zip(self.at, self.dims, offset))

    def device(self, at):
        return (at[0] * 2 + self.core, at[1] * self.dims[2] + at[2])

    def partner(self):
        return (self.at[0] * 2 + 1 - self.core, lax.axis_index("sb"))

    def slot(self, at):
        return (at[0] * self.dims[1] + at[1]) * self.dims[2] + at[2]

    def greet(self):
        barrier = pltpu.get_barrier_semaphore()
        peers = [self.partner()]
        for axis in range(3):
            for step in range(1, self.dims[axis]):
                peers.append(self.device(self.other(axis, step)))
        for peer in peers:
            pl.semaphore_signal(barrier, inc=1, device_id=peer, device_id_type=MESH)
        pl.semaphore_wait(barrier, len(peers))


def pieces(x):
    hi = x.astype(BF)
    rest = x - hi.astype(F32)
    mid = rest.astype(BF)
    low = (rest - mid.astype(F32)).astype(BF)
    return hi, mid, low


def relay_lines(dims, b):
    na, nb, nd = dims
    sends = [((0, b, 0), 2, step) for step in range(1, nd)]
    return sends + [((0, b, 0), 0, step) for step in range(1, na)]


def relay_corners(dims, b):
    na, nb, nd = dims
    sends = [("q", (0, b, d), 0, s) for d in range(1, nd) for s in range(1, na)]
    return sends + [("d", (a, b, 0), 2, s) for a in range(1, na) for s in range(1, nd)]


def first_sends(dims):
    along = [(1, step) for step in range(1, dims[1])]
    across = [(2, step) for step in range(1, dims[2])] + [(0, step) for step in range(1, dims[0])]
    return along, across


def line_order(dims):
    lines = [(a, d) for a in range(dims[0]) for d in range(dims[2])]
    return sorted(lines, key=lambda at: (at[0] != 0) + (at[1] != 0))


def counts(dims):
    na, nb, nd = dims
    along, across = first_sends(dims)
    gathered = 4 * (len(along) + len(across))
    for b in range(nb):
        gathered += 2 * KVH * len(relay_lines(dims, b)) * (b > 0) + KVH * len(relay_corners(dims, b))
    lines = line_order(dims)
    reduced = sum((a != 0) + (d != 0) for a, d in lines) + (na - 1) + (nd - 1) + (nb - 1)
    return gathered, KVH * reduced, (nb - 1) + (nd - 1) + (na - 1)


def whole_kernel(dims, total_keys, tile, q_ref, d_ref, o_ref, lse_ref, k_ref, v_ref,
                 dq_out, dk_out, dv_out,
                 qa, da0, da1, kt, vt, ksend, krecv, auxs, qts, dts, ps, dss, dqs,
                 dk_acc, dv_acc, part, kvs, kvr,
                 r1a, r1b, t1a, t1b, r2a, r2b, t2, r3,
                 send_sem, q_sem, d_sem, kv_send, kv_recv, sum_send, sum_recv,
                 red_send, r1a_sem, r1b_sem, r2a_sem, r2b_sem, r3_sem):
    na, nb, nd = dims
    place = Place(dims)
    pa, pb, pd = place.at
    rows = q_ref.shape[0]
    keys = k_ref.shape[0]
    group = q_ref.shape[1] // KVH
    per_group = QH // KVH
    scale = 1.0 / math.sqrt(HEAD_DIM)
    along, across = first_sends(dims)
    origin = (0, 0, 0)
    block = nb * rows
    cols = block * per_group

    lane = lax.broadcasted_iota(jnp.int32, (rows, HEAD_DIM), 1)
    lse_rows = lse_ref[...].T
    aux = jnp.zeros((rows, HEAD_DIM), F32)
    for head in range(QH):
        at = pl.ds(head * HEAD_DIM, HEAD_DIM)
        product = d_ref[:, at].astype(F32) * o_ref[:, at].astype(F32)
        delta = jnp.sum(product, axis=1, keepdims=True)
        offset = (lse_rows[:, head:head + 1] + math.log(total_keys)) * (1.0 / scale)
        for first, value in ((0, offset), (3 * QH, delta)):
            for n, piece in enumerate(pieces(value)):
                aux = jnp.where(lane == first + 3 * head + n, piece.astype(F32), aux)
    da0[pa, pb, pd, :, pl.ds(group, HEAD_DIM)] = aux.astype(BF)
    da0[pa, pb, pd, :, pl.ds(0, group)] = d_ref[:, pl.ds(0, group)]
    da1[pa, pb, pd] = d_ref[:, pl.ds(group, group)]
    for c in range(KVH):
        qa[c, pa, pb, pd] = q_ref[:, pl.ds(c * group, group)]
    chunk = 128

    def turn(n, total):
        at = pl.ds(pl.multiple_of(n * chunk, chunk), chunk)
        for c in range(KVH):
            head = pl.ds(c * HEAD_DIM, HEAD_DIM)
            kt[0, c, :, at] = k_ref[at, head].T
            vt[0, c, :, at] = v_ref[at, head].T
        return total + jnp.sum(k_ref[at, :].astype(F32), axis=0, keepdims=True)

    key_sum = lax.fori_loop(0, keys // chunk, turn, jnp.zeros((1, KVH * HEAD_DIM), F32))
    row8 = lax.broadcasted_iota(jnp.int32, (8, HEAD_DIM), 0)
    sums = jnp.zeros((8, HEAD_DIM), F32)
    for c in range(KVH):
        sums = jnp.where(row8 == c, key_sum[:, c * HEAD_DIM:(c + 1) * HEAD_DIM], sums)
    ksend[0] = sums

    place.greet()

    partner_copies = []

    def to_partner(src, dst):
        n = len(partner_copies)
        copy = pltpu.make_async_remote_copy(
            src_ref=src, dst_ref=dst, send_sem=kv_send.at[n], recv_sem=kv_recv.at[n],
            device_id=place.partner(), device_id_type=MESH)
        copy.start()
        partner_copies.append(copy)
        return copy

    sum_copies = []

    def send_sums(stage, axis):
        group_of = []
        for step in range(1, dims[axis]):
            n = len(sum_copies)
            copy = pltpu.make_async_remote_copy(
                src_ref=ksend.at[stage], dst_ref=krecv.at[n],
                send_sem=sum_send.at[n], recv_sem=sum_recv.at[n],
                device_id=place.device(place.other(axis, step)), device_id_type=MESH)
            copy.start()
            sum_copies.append(copy)
            group_of.append((copy, n))
        return group_of

    def add_sums(stage, group_of):
        total = ksend[stage]
        for copy, n in group_of:
            copy.wait_recv()
            total = total + krecv[n]
        ksend[stage + 1] = total

    def flat(offset):
        return (offset[0] * nb + offset[1]) * nd + offset[2]

    def places(kind, at, offset):
        c = int(kind[1])
        if kind[0] == "q":
            return qa.at[c, at[0], at[1], at[2]], q_sem.at[c, flat(offset)]
        return (da0, da1)[c].at[at[0], at[1], at[2]], d_sem.at[c, flat(offset)]

    started = []

    def send(kind, offset, axis, step):
        there = list(offset)
        there[axis] = (there[axis] + step) % dims[axis]
        ref, sem = places(kind, place.back(offset), there)
        copy = pltpu.make_async_remote_copy(
            src_ref=ref, dst_ref=ref, send_sem=send_sem.at[len(started)], recv_sem=sem,
            device_id=place.device(place.other(axis, step)), device_id_type=MESH)
        copy.start()
        started.append(copy)

    arrived = set()

    def need(kind, offset):
        if offset == origin or (kind, offset) in arrived:
            return
        arrived.add((kind, offset))
        ref, sem = places(kind, place.back(offset), offset)
        pltpu.make_async_remote_copy(
            src_ref=ref, dst_ref=ref, send_sem=send_sem.at[0], recv_sem=sem,
            device_id=place.partner(), device_id_type=MESH).wait_recv()

    def send_first(c, directions):
        for kind in ("q", "d"):
            for axis, step in directions:
                send(kind + str(c), origin, axis, step)

    def send_line(c, b):
        for kind in ("q", "d"):
            need(kind + str(c), (0, b, 0))
        for kind in ("q", "d"):
            for offset, axis, step in relay_lines(dims, b):
                send(kind + str(c), offset, axis, step)

    def send_corner(c, b):
        for kind, offset, axis, step in relay_corners(dims, b):
            need(kind + str(c), offset)
            send(kind + str(c), offset, axis, step)

    def need_line(c, a, d):
        for b in range(nb):
            for kind in ("q", "d"):
                need(kind + str(c), (a, b, d))

    stage = send_sums(0, 1)
    send_first(0, along + across)
    k_copy = to_partner(kt.at[0], kt.at[1])
    v_copy = to_partner(vt.at[0], vt.at[1])
    send_first(1, across)
    add_sums(0, stage)
    stage = send_sums(1, 2)
    send_corner(0, 0)
    if nb > 1:
        send_line(0, 1)
    add_sums(1, stage)
    stage = send_sums(2, 0)
    for b in range(2, nb):
        send_line(0, b)
    add_sums(2, stage)
    sum_copy = to_partner(ksend.at[3], ksend.at[4])
    send_first(1, along)
    k_copy.wait_recv()
    v_copy.wait_recv()
    sum_copy.wait_recv()
    k_copy.wait_send()
    mean = (ksend[3] + ksend[4]) * (1.0 / total_keys)
    means = []
    for c in range(KVH):
        means.append(jnp.broadcast_to(mean[c:c + 1], (HEAD_DIM, HEAD_DIM)).T)

    def smooth(n, carry):
        at = pl.ds(pl.multiple_of(n * chunk, chunk), chunk)
        for side in range(2):
            for c in range(KVH):
                kt[side, c, :, at] = (kt[side, c, :, at].astype(F32) - means[c]).astype(BF)
        return carry

    lax.fori_loop(0, keys // chunk, smooth, 0)

    nt = (((1,), (1,)), ((), ()))
    tiles = keys // tile
    lane_b = lax.broadcasted_iota(jnp.int32, (block, HEAD_DIM), 1)

    def line_at(a, d):
        return (pa + na - a) % na, (pd + nd - d) % nd

    def prepare(n, c, a, d):
        la, ld = line_at(a, d)
        aux_rows = da0[la, :, ld, :, pl.ds(group, HEAD_DIM)].reshape(block, HEAD_DIM)
        for g in range(per_group):
            head = pl.ds(g * HEAD_DIM, HEAD_DIM)
            here = pl.ds(g * block, block)
            low = 3 * (c * per_group + g)
            keep = (lane_b >= low) & (lane_b < low + 3)
            low = low + 3 * QH
            keep = keep | ((lane_b >= low) & (lane_b < low + 3))
            auxs[n, here, :] = jnp.where(keep, aux_rows.astype(F32), 0.0).astype(BF)
            qts[n, :, here] = qa[c, la, :, ld, :, head].reshape(block, HEAD_DIM).T
            dts[n, :, here] = (da0, da1)[c][la, :, ld, :, head].reshape(block, HEAD_DIM).T

    def scores(n, m, c, a, d, side, t):
        la, ld = line_at(a, d)
        at = pl.ds(t * tile, tile)
        key_row = lax.broadcasted_iota(jnp.int32, (HEAD_DIM, tile), 0)
        pick_s = jnp.where(key_row < 3 * QH, -1.0, 0.0).astype(BF)
        pick_d = jnp.where((key_row >= 3 * QH) & (key_row < 6 * QH), -1.0, 0.0).astype(BF)
        kk = jnp.concatenate([kt[side, c, :, at], pick_s], 0)
        vv = jnp.concatenate([vt[side, c, :, at], pick_d], 0)
        for g in range(per_group):
            head = pl.ds(g * HEAD_DIM, HEAD_DIM)
            here = pl.ds(g * block, block)
            qh = qa[c, la, :, ld, :, head].reshape(block, HEAD_DIM)
            dh = (da0, da1)[c][la, :, ld, :, head].reshape(block, HEAD_DIM)
            s = jnp.dot(jnp.concatenate([qh, auxs[n, here, :]], 1), kk, preferred_element_type=F32)
            dp = jnp.dot(jnp.concatenate([dh, auxs[n, here, :]], 1), vv, preferred_element_type=F32)
            prob = jnp.exp2(s * (scale * math.log2(math.e)))
            ps[m, here, :] = prob.astype(BF)
            dss[m, here, :] = (prob * dp).astype(BF)

    def products(n, m, c, side, t, first_line, first_tile):
        at = pl.ds(t * tile, tile)
        dv = jnp.dot(dts[n], ps[m], preferred_element_type=F32)
        dk = jnp.dot(qts[n], dss[m], preferred_element_type=F32)
        dq = lax.dot_general(kt[side, c, :, at], dss[m], nt, preferred_element_type=F32)
        if first_line:
            dv_acc[side, c, :, at] = dv
            dk_acc[side, c, :, at] = dk
        else:
            dv_acc[side, c, :, at] += dv
            dk_acc[side, c, :, at] += dk
        if first_tile:
            dqs[n] = dq
        else:
            dqs[n] += dq

    def finish(n, c, a, d):
        la, ld = line_at(a, d)
        for g in range(per_group):
            here = pl.ds(g * block, block)
            piece = (dqs[n, :, here] * scale).astype(BF).T
            part[c, la, :, ld, :, pl.ds(g * HEAD_DIM, HEAD_DIM)] = piece.reshape(nb, rows, HEAD_DIM)

    mid = group // 2
    left, right = pl.ds(0, mid), pl.ds(mid, mid)
    reduced = []

    def red(src, dst, sem, to):
        copy = pltpu.make_async_remote_copy(
            src_ref=src, dst_ref=dst, send_sem=red_send.at[len(reduced)], recv_sem=sem,
            device_id=place.device(to), device_id_type=MESH)
        copy.start()
        reduced.append(copy)

    def landed(ref, sem):
        pltpu.make_async_remote_copy(
            src_ref=ref, dst_ref=ref, send_sem=red_send.at[0], recv_sem=sem,
            device_id=place.partner(), device_id_type=MESH).wait_recv()

    def stage1(c, a, d):
        la, ld = line_at(a, d)
        if d:
            s = nd - d
            red(part.at[c, la, :, ld, :, left], r1a.at[c, s - 1, la],
                r1a_sem.at[c, s - 1, a], place.other(2, s))
        if a:
            s = na - a
            red(part.at[c, la, :, ld, :, right], r1b.at[c, s - 1, ld],
                r1b_sem.at[c, s - 1, d], place.other(0, s))

    def sum_left(c, a):
        la, _ = line_at(a, 0)
        total = part[c, la, :, pd, :, left].astype(F32)
        for s in range(nd - 1):
            landed(r1a.at[c, s, la], r1a_sem.at[c, s, a])
            total = total + r1a[c, s, la].astype(F32)
        return total

    def sum_right(c, d):
        _, ld = line_at(0, d)
        total = part[c, pa, :, ld, :, right].astype(F32)
        for s in range(na - 1):
            landed(r1b.at[c, s, ld], r1b_sem.at[c, s, d])
            total = total + r1b[c, s, ld].astype(F32)
        return total

    def stage2(c):
        for a in range(1, na):
            t1a[c, a] = sum_left(c, a).astype(BF)
            s = na - a
            red(t1a.at[c, a], r2a.at[c, s - 1], r2a_sem.at[c, s - 1], place.other(0, s))
        for d in range(1, nd):
            t1b[c, d] = sum_right(c, d).astype(BF)
            s = nd - d
            red(t1b.at[c, d], r2b.at[c, s - 1], r2b_sem.at[c, s - 1], place.other(2, s))

    def stage3(c):
        total = sum_left(c, 0)
        for s in range(na - 1):
            landed(r2a.at[c, s], r2a_sem.at[c, s])
            total = total + r2a[c, s].astype(F32)
        t2[c, :, :, left] = total.astype(BF)
        total = sum_right(c, 0)
        for s in range(nd - 1):
            landed(r2b.at[c, s], r2b_sem.at[c, s])
            total = total + r2b[c, s].astype(F32)
        t2[c, :, :, right] = total.astype(BF)
        for s in range(1, nb):
            to = place.other(1, s)
            red(t2.at[c, to[1]], r3.at[c, s - 1], r3_sem.at[c, s - 1], to)

    def last(c):
        total = t2[c, pb].astype(F32)
        for s in range(nb - 1):
            landed(r3.at[c, s], r3_sem.at[c, s])
            total = total + r3[c, s].astype(F32)
        dq_out[:, pl.ds(c * group, group)] = total

    kv = []

    def share(c):
        for which, acc, factor in ((0, dk_acc, scale), (1, dv_acc, 1.0)):
            kvs[c, which] = (acc[1, c] * factor).astype(BF)
            kv.append(to_partner(kvs.at[c, which], kvr.at[c, which]))

    def collect(c):
        head = pl.ds(c * HEAD_DIM, HEAD_DIM)
        for which, acc, factor, out in ((0, dk_acc, scale, dk_out), (1, dv_acc, 1.0, dv_out)):
            kv[2 * c + which].wait_recv()
            total = acc[0, c] * factor + kvr[c, which].astype(F32)
            out[:, head] = total.astype(BF).T

    lines = line_order(dims)
    orders = (lines, lines[1:][::-1] + lines[:1])
    events = {}

    def plan(c, n, half, action):
        events.setdefault((c, min(n, len(lines) - 1), half), []).append(action)

    for b in range(1, nb):
        plan(0, 0 if b < 2 else 1, b < 2, functools.partial(send_corner, 0, b))
        plan(0, 1, 1, functools.partial(send_line, 1, b))
    for b in range(nb):
        plan(0, 2, 1, functools.partial(send_corner, 1, b))
    plan(1, 1, 1, lambda: stage2(0))
    plan(1, 2, 1, lambda: stage3(0))
    plan(1, 3, 1, lambda: stage2(1))

    steps = [(side, t) for side in (1, 0) for t in range(tiles)]
    pending = None
    count = 0
    ended = None
    for c in range(KVH):
        for n, (a, d) in enumerate(orders[c]):
            for action in events.get((c, n, 0), []):
                action()
            need_line(c, a, d)
            if a or d:
                need_line(0, a, d)
            slot = n % 2
            prepare(slot, c, a, d)
            for i, (side, t) in enumerate(steps):
                if i == len(steps) // 2:
                    for action in events.get((c, n, 1), []):
                        action()
                scores(slot, count % 2, c, a, d, side, t)
                if pending is not None:
                    products(*pending)
                    pending = None
                if ended is not None:
                    finish(*ended)
                    stage1(*ended[1:])
                    ended = None
                pending = (slot, count % 2, c, side, t, n == 0, i == 0)
                count += 1
            ended = (slot, c, a, d)
        products(*pending)
        finish(*ended)
        pending = None
        stage1(*ended[1:])
        ended = None
        share(c)
    stage3(1)
    collect(0)
    last(0)
    collect(1)
    last(1)
    for copy in started + partner_copies[1:] + sum_copies + reduced:
        copy.wait_send()


def local(dims, q, d, o, lse, k, v):
    na, nb, nd = dims
    members = na * nb * nd
    rows, width = q.shape
    keys, kw = k.shape
    group, mid = width // KVH, width // KVH // 2
    cols = nb * rows * (QH // KVH)
    tile = min(512, keys)
    gathered, reduced, summed = counts(dims)
    vmem = pl.BlockSpec(memory_space=pltpu.VMEM)
    ma, mb, md = max(na - 1, 1), max(nb - 1, 1), max(nd - 1, 1)
    sem = pltpu.SemaphoreType.DMA
    return pl.pallas_call(
        functools.partial(whole_kernel, dims, keys * members * 2, tile),
        name="whole",
        out_shape=(
            jax.ShapeDtypeStruct((rows, width), F32),
            jax.ShapeDtypeStruct((keys, kw), BF),
            jax.ShapeDtypeStruct((keys, kw), BF),
        ),
        in_specs=[vmem] * 6,
        out_specs=(vmem,) * 3,
        scratch_shapes=[
            pltpu.VMEM((KVH, na, nb, nd, rows, group), BF),
            pltpu.VMEM((na, nb, nd, rows, group + HEAD_DIM), BF),
            pltpu.VMEM((na, nb, nd, rows, group), BF),
            pltpu.VMEM((2, KVH, HEAD_DIM, keys), BF),
            pltpu.VMEM((2, KVH, HEAD_DIM, keys), BF),
            pltpu.VMEM((5, 8, HEAD_DIM), F32),
            pltpu.VMEM((max(summed, 1), 8, HEAD_DIM), F32),
            pltpu.VMEM((2, cols, HEAD_DIM), BF),
            pltpu.VMEM((2, HEAD_DIM, cols), BF),
            pltpu.VMEM((2, HEAD_DIM, cols), BF),
            pltpu.VMEM((2, cols, tile), BF),
            pltpu.VMEM((2, cols, tile), BF),
            pltpu.VMEM((2, HEAD_DIM, cols), F32),
            pltpu.VMEM((2, KVH, HEAD_DIM, keys), F32),
            pltpu.VMEM((2, KVH, HEAD_DIM, keys), F32),
            pltpu.VMEM((KVH, na, nb, nd, rows, group), BF),
            pltpu.VMEM((KVH, 2, HEAD_DIM, keys), BF),
            pltpu.VMEM((KVH, 2, HEAD_DIM, keys), BF),
            pltpu.VMEM((KVH, md, na, nb, rows, mid), BF),
            pltpu.VMEM((KVH, ma, nd, nb, rows, mid), BF),
            pltpu.VMEM((KVH, na, nb, rows, mid), BF),
            pltpu.VMEM((KVH, nd, nb, rows, mid), BF),
            pltpu.VMEM((KVH, ma, nb, rows, mid), BF),
            pltpu.VMEM((KVH, md, nb, rows, mid), BF),
            pltpu.VMEM((KVH, nb, rows, group), BF),
            pltpu.VMEM((KVH, mb, rows, group), BF),
            sem((gathered,)),
            sem((KVH, members)),
            sem((KVH, members)),
            sem((3 + 2 * KVH,)),
            sem((3 + 2 * KVH,)),
            sem((max(summed, 1),)),
            sem((max(summed, 1),)),
            sem((reduced,)),
            sem((KVH, md, na)),
            sem((KVH, ma, nd)),
            sem((KVH, ma)),
            sem((KVH, md)),
            sem((KVH, mb)),
        ],
        compiler_params=pltpu.CompilerParams(
            collective_id=0, has_side_effects=True, vmem_limit_bytes=60 * 1024 * 1024),
    )(q, d, o, lse.T, k, v)


def solution(mesh):
    dims = grid_of(mesh.shape["sa"], mesh.shape["sb"])
    spec = P(("sa", "sb"), None)
    return jax.shard_map(functools.partial(local, dims), mesh=mesh, in_specs=(spec,) * 6,
                         out_specs=(spec,) * 3, check_vma=False)
```

time: 74.2 us -> 60.5 us (0.82)
  Pallas kernels: 67.7 us -> 55.3 us
  local copies, waits for them, and re-layouts: 5.66 us -> 4.29 us
    pallas_call x1, Pallas kernels: 67.7 us -> 55.3 us  [local(): pl.pallas_call(functools.partial(whole_kernel, dims, keys * members * 2,...]
    unnamed x6 -> x5, local copies, waits for them, and re-layouts: 5.66 us -> 4.29 us
where the time goes in v1:
time: 60.5 us; the launch traced here: 60.3 us
  Pallas kernels  55.3 us (91%)
  local copies, waits for them, and re-layouts  4.29 us (7%)
  between operations  0.64 us (1%)
    pallas_call x1, Pallas kernels, local(): pl.pallas_call(functools.partial(whole_kernel, dims, keys * members * 2,...  55.3 us
    unnamed x5, local copies, waits for them, and re-layouts  4.29 us

profile of v1, /device:TPU:0, one launch (start us, length us, event | category | flops | bytes accessed | tf_op | source)
XLA Modules:
  0.0 60.3 jit_solution(11722180845827820033)
XLA Ops:
  0.6 55.3 %whole.1 = (f32[32,1024]{1,0:T(8,128)}, bf16[1024,256]{1,0:T(8,128)(2,1)}, bf16[1024,256]{1,0:T(8,128)(2,1)}) custom-call(bf16[32,1024]{1,0:T(8,128)(2,1)} %q_ref.1, bf16[32,1024]{1,0:T(8,128)(2,1)} %d_ref.1, bf16[32,1024]{1,0:T(8,128)(2,1)} %o_ref.1, f32[8,32]{1,0:T(8,128)} %bitcast.1, bf16[1024,256]{1,0:T(8,128)(2,1)} %k_ref.1, bf16[1024,256]{1,0:T(8,128)(2,1)} %v_ref.1), custom_call_target="tpu_custom_call" | custom-call | tf_op jit(solution)/shard_map/whole/pallas_call | solution.py:502
  56.0 1.6 %copy.12 = f32[32,1024]{1,0:T(8,128)} copy(f32[32,1024]{1,0:T(8,128)} %get-tuple-element.6) | data formatting | bytes 262144
  57.5 0.0 copy-start
  57.5 1.9 %copy.13 = bf16[1024,256]{1,0:T(8,128)(2,1)} copy(bf16[1024,256]{1,0:T(8,128)(2,1)} %get-tuple-element.7) | data formatting | bytes 1048576
  59.5 0.0 copy-done
  59.5 0.8 %copy.14 = bf16[1024,256]{1,0:T(8,128)(2,1)} copy(bf16[1024,256]{1,0:T(8,128)(2,1)S(1)} %copy-done) | data formatting | bytes 1048576
Async XLA Ops:
  57.5 1.9 %copy-start = (bf16[1024,256]{1,0:T(8,128)(2,1)S(1)}, bf16[1024,256]{1,0:T(8,128)(2,1)}, u32[]{:S(2)}) copy-start(bf16[1024,256]{1,0:T(8,128)(2,1)} %get-tuple-element.8) | copy-start | bytes 1572868

commit v2 on v1

--- a/solution.py
+++ b/solution.py
@@ -34,6 +34,9 @@
         at[axis] = (at[axis] + step) % self.dims[axis]
         return tuple(at)
 
+    def across(self, a, d):
+        return ((self.at[0] + a) % self.dims[0], self.at[1], (self.at[2] + d) % self.dims[2])
+
     def back(self, offset):
         return tuple((p + n - o) % n for p, n, o in zip(self.at, self.dims, offset))
 
@@ -52,6 +55,9 @@
         for axis in range(3):
             for step in range(1, self.dims[axis]):
                 peers.append(self.device(self.other(axis, step)))
+        for a in range(1, self.dims[0]):
+            for d in range(1, self.dims[2]):
+                peers.append(self.device(self.across(a, d)))
         for peer in peers:
             pl.semaphore_signal(barrier, inc=1, device_id=peer, device_id_type=MESH)
         pl.semaphore_wait(barrier, len(peers))
@@ -96,7 +102,7 @@
         gathered += 2 * KVH * len(relay_lines(dims, b)) * (b > 0) + KVH * len(relay_corners(dims, b))
     lines = line_order(dims)
     reduced = sum((a != 0) + (d != 0) for a, d in lines) + (na - 1) + (nd - 1) + (nb - 1)
-    return gathered, KVH * reduced, (nb - 1) + (nd - 1) + (na - 1)
+    return gathered, KVH * reduced, nb - 1 + na * nd - 1
 
 
 def whole_kernel(dims, total_keys, tile, q_ref, d_ref, o_ref, lse_ref, k_ref, v_ref,
@@ -119,6 +125,113 @@
     block = nb * rows
     cols = block * per_group
 
+    da1[pa, pb, pd] = d_ref[:, pl.ds(group, group)]
+    for c in range(KVH):
+        qa[c, pa, pb, pd] = q_ref[:, pl.ds(c * group, group)]
+    chunk = 128
+
+    def add_rows(n, total):
+        at = pl.ds(pl.multiple_of(n * chunk, chunk), chunk)
+        return total + jnp.sum(k_ref[at, :].astype(F32), axis=0, keepdims=True)
+
+    key_sum = lax.fori_loop(0, keys // chunk, add_rows, jnp.zeros((1, KVH * HEAD_DIM), F32))
+    row8 = lax.broadcasted_iota(jnp.int32, (8, HEAD_DIM), 0)
+    sums = jnp.zeros((8, HEAD_DIM), F32)
+    for c in range(KVH):
+        sums = jnp.where(row8 == c, key_sum[:, c * HEAD_DIM:(c + 1) * HEAD_DIM], sums)
+    ksend[0] = sums
+
+    place.greet()
+
+    partner_copies = []
+
+    def to_partner(src, dst):
+        n = len(partner_copies)
+        copy = pltpu.make_async_remote_copy(
+            src_ref=src, dst_ref=dst, send_sem=kv_send.at[n], recv_sem=kv_recv.at[n],
+            device_id=place.partner(), device_id_type=MESH)
+        copy.start()
+        partner_copies.append(copy)
+        return copy
+
+    sum_copies = []
+
+    def send_sums(stage, peers):
+        group_of = []
+        for peer in peers:
+            n = len(sum_copies)
+            copy = pltpu.make_async_remote_copy(
+                src_ref=ksend.at[stage], dst_ref=krecv.at[n],
+                send_sem=sum_send.at[n], recv_sem=sum_recv.at[n],
+                device_id=place.device(peer), device_id_type=MESH)
+            copy.start()
+            sum_copies.append(copy)
+            group_of.append((copy, n))
+        return group_of
+
+    def add_sums(stage, group_of):
+        total = ksend[stage]
+        for copy, n in group_of:
+            copy.wait_recv()
+            total = total + krecv[n]
+        ksend[stage + 1] = total
+
+    def flat(offset):
+        return (offset[0] * nb + offset[1]) * nd + offset[2]
+
+    def places(kind, at, offset):
+        c = int(kind[1])
+        if kind[0] == "q":
+            return qa.at[c, at[0], at[1], at[2]], q_sem.at[c, flat(offset)]
+        return (da0, da1)[c].at[at[0], at[1], at[2]], d_sem.at[c, flat(offset)]
+
+    started = []
+
+    def send(kind, offset, axis, step):
+        there = list(offset)
+        there[axis] = (there[axis] + step) % dims[axis]
+        ref, sem = places(kind, place.back(offset), there)
+        copy = pltpu.make_async_remote_copy(
+            src_ref=ref, dst_ref=ref, send_sem=send_sem.at[len(started)], recv_sem=sem,
+            device_id=place.device(place.other(axis, step)), device_id_type=MESH)
+        copy.start()
+        started.append(copy)
+
+    arrived = set()
+
+    def need(kind, offset):
+        if offset == origin or (kind, offset) in arrived:
+            return
+        arrived.add((kind, offset))
+        ref, sem = places(kind, place.back(offset), offset)
+        pltpu.make_async_remote_copy(
+            src_ref=ref, dst_ref=ref, send_sem=send_sem.at[0], recv_sem=sem,
+            device_id=place.partner(), device_id_type=MESH).wait_recv()
+
+    def send_first(kinds, directions):
+        for kind in kinds:
+            for axis, step in directions:
+                send(kind, origin, axis, step)
+
+    def send_line(c, b):
+        for kind in ("q", "d"):
+            need(kind + str(c), (0, b, 0))
+        for kind in ("q", "d"):
+            for offset, axis, step in relay_lines(dims, b):
+                send(kind + str(c), offset, axis, step)
+
+    def send_corner(c, b):
+        for kind, offset, axis, step in relay_corners(dims, b):
+            need(kind + str(c), offset)
+            send(kind + str(c), offset, axis, step)
+
+    def need_line(c, a, d):
+        for b in range(nb):
+            for kind in ("q", "d"):
+                need(kind + str(c), (a, b, d))
+
+    stage = send_sums(0, [place.other(1, step) for step in range(1, nb)])
+    send_first(("q0",), along + across)
     lane = lax.broadcasted_iota(jnp.int32, (rows, HEAD_DIM), 1)
     lse_rows = lse_ref[...].T
     aux = jnp.zeros((rows, HEAD_DIM), F32)
@@ -132,149 +245,44 @@
                 aux = jnp.where(lane == first + 3 * head + n, piece.astype(F32), aux)
     da0[pa, pb, pd, :, pl.ds(group, HEAD_DIM)] = aux.astype(BF)
     da0[pa, pb, pd, :, pl.ds(0, group)] = d_ref[:, pl.ds(0, group)]
-    da1[pa, pb, pd] = d_ref[:, pl.ds(group, group)]
-    for c in range(KVH):
-        qa[c, pa, pb, pd] = q_ref[:, pl.ds(c * group, group)]
-    chunk = 128
-
-    def turn(n, total):
+    send_first(("d0",), along + across)
+
+    def turn(n, carry):
         at = pl.ds(pl.multiple_of(n * chunk, chunk), chunk)
         for c in range(KVH):
             head = pl.ds(c * HEAD_DIM, HEAD_DIM)
             kt[0, c, :, at] = k_ref[at, head].T
             vt[0, c, :, at] = v_ref[at, head].T
-        return total + jnp.sum(k_ref[at, :].astype(F32), axis=0, keepdims=True)
-
-    key_sum = lax.fori_loop(0, keys // chunk, turn, jnp.zeros((1, KVH * HEAD_DIM), F32))
-    row8 = lax.broadcasted_iota(jnp.int32, (8, HEAD_DIM), 0)
-    sums = jnp.zeros((8, HEAD_DIM), F32)
-    for c in range(KVH):
-        sums = jnp.where(row8 == c, key_sum[:, c * HEAD_DIM:(c + 1) * HEAD_DIM], sums)
-    ksend[0] = sums
-
-    place.greet()
-
-    partner_copies = []
-
-    def to_partner(src, dst):
-        n = len(partner_copies)
-        copy = pltpu.make_async_remote_copy(
-            src_ref=src, dst_ref=dst, send_sem=kv_send.at[n], recv_sem=kv_recv.at[n],
-            device_id=place.partner(), device_id_type=MESH)
-        copy.start()
-        partner_copies.append(copy)
-        return copy
-
-    sum_copies = []
-
-    def send_sums(stage, axis):
-        group_of = []
-        for step in range(1, dims[axis]):
-            n = len(sum_copies)
-            copy = pltpu.make_async_remote_copy(
-                src_ref=ksend.at[stage], dst_ref=krecv.at[n],
-                send_sem=sum_send.at[n], recv_sem=sum_recv.at[n],
-                device_id=place.device(place.other(axis, step)), device_id_type=MESH)
-            copy.start()
-            sum_copies.append(copy)
-            group_of.append((copy, n))
-        return group_of
-
-    def add_sums(stage, group_of):
-        total = ksend[stage]
-        for copy, n in group_of:
-            copy.wait_recv()
-            total = total + krecv[n]
-        ksend[stage + 1] = total
-
-    def flat(offset):
-        return (offset[0] * nb + offset[1]) * nd + offset[2]
-
-    def places(kind, at, offset):
-        c = int(kind[1])
-        if kind[0] == "q":
-            return qa.at[c, at[0], at[1], at[2]], q_sem.at[c, flat(offset)]
-        return (da0, da1)[c].at[at[0], at[1], at[2]], d_sem.at[c, flat(offset)]
-
-    started = []
-
-    def send(kind, offset, axis, step):
-        there = list(offset)
-        there[axis] = (there[axis] + step) % dims[axis]
-        ref, sem = places(kind, place.back(offset), there)
-        copy = pltpu.make_async_remote_copy(
-            src_ref=ref, dst_ref=ref, send_sem=send_sem.at[len(started)], recv_sem=sem,
-            device_id=place.device(place.other(axis, step)), device_id_type=MESH)
-        copy.start()
-        started.append(copy)
-
-    arrived = set()
-
-    def need(kind, offset):
-        if offset == origin or (kind, offset) in arrived:
-            return
-        arrived.add((kind, offset))
-        ref, sem = places(kind, place.back(offset), offset)
-        pltpu.make_async_remote_copy(
-            src_ref=ref, dst_ref=ref, send_sem=send_sem.at[0], recv_sem=sem,
-            device_id=place.partner(), device_id_type=MESH).wait_recv()
-
-    def send_first(c, directions):
-        for kind in ("q", "d"):
-            for axis, step in directions:
-                send(kind + str(c), origin, axis, step)
-
-    def send_line(c, b):
-        for kind in ("q", "d"):
-            need(kind + str(c), (0, b, 0))
-        for kind in ("q", "d"):
-            for offset, axis, step in relay_lines(dims, b):
-                send(kind + str(c), offset, axis, step)
-
-    def send_corner(c, b):
-        for kind, offset, axis, step in relay_corners(dims, b):
-            need(kind + str(c), offset)
-            send(kind + str(c), offset, axis, step)
-
-    def need_line(c, a, d):
-        for b in range(nb):
-            for kind in ("q", "d"):
-                need(kind + str(c), (a, b, d))
-
-    stage = send_sums(0, 1)
-    send_first(0, along + across)
+        return carry
+
+    lax.fori_loop(0, keys // chunk, turn, 0)
     k_copy = to_partner(kt.at[0], kt.at[1])
     v_copy = to_partner(vt.at[0], vt.at[1])
-    send_first(1, across)
     add_sums(0, stage)
-    stage = send_sums(1, 2)
+    stage = send_sums(1, [place.across(a, d) for a, d in line_order(dims)[1:]])
+    send_first(("q1", "d1"), across)
     send_corner(0, 0)
-    if nb > 1:
-        send_line(0, 1)
     add_sums(1, stage)
-    stage = send_sums(2, 0)
-    for b in range(2, nb):
+    sum_copy = to_partner(ksend.at[2], ksend.at[3])
+    for b in range(1, nb):
         send_line(0, b)
-    add_sums(2, stage)
-    sum_copy = to_partner(ksend.at[3], ksend.at[4])
-    send_first(1, along)
+    send_first(("q1", "d1"), along)
     k_copy.wait_recv()
     v_copy.wait_recv()
     sum_copy.wait_recv()
     k_copy.wait_send()
-    mean = (ksend[3] + ksend[4]) * (1.0 / total_keys)
-    means = []
-    for c in range(KVH):
-        means.append(jnp.broadcast_to(mean[c:c + 1], (HEAD_DIM, HEAD_DIM)).T)
-
-    def smooth(n, carry):
-        at = pl.ds(pl.multiple_of(n * chunk, chunk), chunk)
-        for side in range(2):
-            for c in range(KVH):
-                kt[side, c, :, at] = (kt[side, c, :, at].astype(F32) - means[c]).astype(BF)
-        return carry
-
-    lax.fori_loop(0, keys // chunk, smooth, 0)
+    mean = (ksend[2] + ksend[3]) * (1.0 / total_keys)
+
+    def smooth(c):
+        mean_t = jnp.broadcast_to(mean[c:c + 1], (HEAD_DIM, HEAD_DIM)).T
+
+        def part_of(n, carry):
+            at = pl.ds(pl.multiple_of(n * chunk, chunk), chunk)
+            for side in range(2):
+                kt[side, c, :, at] = (kt[side, c, :, at].astype(F32) - mean_t).astype(BF)
+            return carry
+
+        lax.fori_loop(0, keys // chunk, part_of, 0)
 
     nt = (((1,), (1,)), ((), ()))
     tiles = keys // tile
@@ -429,55 +437,57 @@
             out[:, head] = total.astype(BF).T
 
     lines = line_order(dims)
-    orders = (lines, lines[1:][::-1] + lines[:1])
+    far = [at for at in lines if at[0] and at[1]]
+    straight = [at for at in lines if bool(at[0]) != bool(at[1])]
+    near_y = [at for at in straight if at[0]]
+    near_x = [at for at in straight if at[1]]
+    orders = (lines, near_y + far + near_x + lines[:1])
     events = {}
-
-    def plan(c, n, half, action):
-        events.setdefault((c, min(n, len(lines) - 1), half), []).append(action)
+    half = len(lines) * 2 * tiles
+
+    def plan(k, action, *args):
+        events.setdefault(k * half // 16, []).append(functools.partial(action, *args))
 
     for b in range(1, nb):
-        plan(0, 0 if b < 2 else 1, b < 2, functools.partial(send_corner, 0, b))
-        plan(0, 1, 1, functools.partial(send_line, 1, b))
+        plan(min(b + 1, 4), send_corner, 0, b)
+        plan(min(6 + 3 * b, 15), send_line, 1, b)
     for b in range(nb):
-        plan(0, 2, 1, functools.partial(send_corner, 1, b))
-    plan(1, 1, 1, lambda: stage2(0))
-    plan(1, 2, 1, lambda: stage3(0))
-    plan(1, 3, 1, lambda: stage2(1))
+        plan(5 if b == 0 else min(13 + 2 * b, 18), send_corner, 1, b)
+    for n, (a, d) in enumerate(lines[1:]):
+        plan(min(19 + n, 22), stage1, 0, a, d)
+    plan(28, stage2, 0)
+    plan(30, stage2, 1)
 
     steps = [(side, t) for side in (1, 0) for t in range(tiles)]
-    pending = None
+    pending = ended = None
     count = 0
-    ended = None
     for c in range(KVH):
+        smooth(c)
         for n, (a, d) in enumerate(orders[c]):
-            for action in events.get((c, n, 0), []):
-                action()
-            need_line(c, a, d)
-            if a or d:
-                need_line(0, a, d)
             slot = n % 2
-            prepare(slot, c, a, d)
             for i, (side, t) in enumerate(steps):
-                if i == len(steps) // 2:
-                    for action in events.get((c, n, 1), []):
-                        action()
+                for action in events.get(count, []):
+                    action()
+                if i == 0:
+                    need_line(c, a, d)
+                    need_line(0, a, d)
+                    prepare(slot, c, a, d)
                 scores(slot, count % 2, c, a, d, side, t)
                 if pending is not None:
                     products(*pending)
-                    pending = None
                 if ended is not None:
                     finish(*ended)
-                    stage1(*ended[1:])
-                    ended = None
+                    if c:
+                        stage1(*ended[1:])
                 pending = (slot, count % 2, c, side, t, n == 0, i == 0)
+                ended = None
                 count += 1
             ended = (slot, c, a, d)
         products(*pending)
         finish(*ended)
-        pending = None
-        stage1(*ended[1:])
-        ended = None
+        pending = ended = None
         share(c)
+    stage3(0)
     stage3(1)
     collect(0)
     last(0)
@@ -515,7 +525,7 @@
             pltpu.VMEM((na, nb, nd, rows, group), BF),
             pltpu.VMEM((2, KVH, HEAD_DIM, keys), BF),
             pltpu.VMEM((2, KVH, HEAD_DIM, keys), BF),
-            pltpu.VMEM((5, 8, HEAD_DIM), F32),
+            pltpu.VMEM((4, 8, HEAD_DIM), F32),
             pltpu.VMEM((max(summed, 1), 8, HEAD_DIM), F32),
             pltpu.VMEM((2, cols, HEAD_DIM), BF),
             pltpu.VMEM((2, HEAD_DIM, cols), BF),

time: 60.5 us -> 58.2 us (0.962)
  Pallas kernels: 55.3 us -> 53.1 us
    pallas_call x1, Pallas kernels: 55.3 us -> 53.1 us  [local(): pl.pallas_call(functools.partial(whole_kernel, dims, keys * members * 2,...]
where the time goes in v2:
time: 58.2 us; the launch traced here: 58 us
  Pallas kernels  53.1 us (91%)
  local copies, waits for them, and re-layouts  4.29 us (7%)
  between operations  0.64 us (1%)
    pallas_call x1, Pallas kernels, local(): pl.pallas_call(functools.partial(whole_kernel, dims, keys * members * 2,...  53.1 us
    unnamed x5, local copies, waits for them, and re-layouts  4.29 us

profile of v2, /device:TPU:0, one launch (start us, length us, event | category | flops | bytes accessed | tf_op | source)
XLA Modules:
  0.0 58.0 jit_solution(13608330166215788874)
XLA Ops:
  0.6 53.1 %whole.1 = (f32[32,1024]{1,0:T(8,128)}, bf16[1024,256]{1,0:T(8,128)(2,1)}, bf16[1024,256]{1,0:T(8,128)(2,1)}) custom-call(bf16[32,1024]{1,0:T(8,128)(2,1)} %q_ref.1, bf16[32,1024]{1,0:T(8,128)(2,1)} %d_ref.1, bf16[32,1024]{1,0:T(8,128)(2,1)} %o_ref.1, f32[8,32]{1,0:T(8,128)} %bitcast.1, bf16[1024,256]{1,0:T(8,128)(2,1)} %k_ref.1, bf16[1024,256]{1,0:T(8,128)(2,1)} %v_ref.1), custom_call_target="tpu_custom_call" | custom-call | tf_op jit(solution)/shard_map/whole/pallas_call | solution.py:512
  53.7 1.6 %copy.12 = f32[32,1024]{1,0:T(8,128)} copy(f32[32,1024]{1,0:T(8,128)} %get-tuple-element.6) | data formatting | bytes 262144
  55.3 0.0 copy-start
  55.3 1.9 %copy.13 = bf16[1024,256]{1,0:T(8,128)(2,1)} copy(bf16[1024,256]{1,0:T(8,128)(2,1)} %get-tuple-element.7) | data formatting | bytes 1048576
  57.2 0.0 copy-done
  57.2 0.8 %copy.14 = bf16[1024,256]{1,0:T(8,128)(2,1)} copy(bf16[1024,256]{1,0:T(8,128)(2,1)S(1)} %copy-done) | data formatting | bytes 1048576
Async XLA Ops:
  55.3 1.9 %copy-start = (bf16[1024,256]{1,0:T(8,128)(2,1)S(1)}, bf16[1024,256]{1,0:T(8,128)(2,1)}, u32[]{:S(2)}) copy-start(bf16[1024,256]{1,0:T(8,128)(2,1)} %get-tuple-element.8) | copy-start | bytes 1572868
